TPU v7x, 32 devices: a whole 2x2x4 slice. The times are simulated.
32 devices in a mesh: row: 8 (over y, x, core), col: 4 (over z).
Axes of the slice: x: 2, y: 2, z: 4, core: 2. Of those that a mesh axis runs over, the one named last changes fastest.
Arguments:
- blocks: bfloat16 [8, 4, 368, 128, 128], P('row', 'col'), may hold values from -0.125 to 0.125
- block_rows: int32 [8, 4, 368], P('row', 'col'), may hold values from 0 to 31, as said below
- block_cols: int32 [8, 4, 368], P('row', 'col'), may hold values from 0 to 63
- counts: int32 [8, 4], P('row', 'col'), may hold values from 1 to 368, as said below
- features: bfloat16 [32768, 256], P(('col', 'row')), may hold values from -6 to 6
Outputs:
- aggregated: bfloat16 [32768, 256], P(('row', 'col'))
Inputs may be any that keep to these rules, and one draw needn't show every extreme that they name: `block_rows`: within one tile the live slots name distinct pairs of block row and block column. `counts`: some tile holds exactly 368 live blocks in every draw.
All inputs are finite; a program needn't handle non-finite values.
Results may differ from a plain program's by a relative error of at most 0.013.
Values may be sent and summed in bfloat16 or wider, within the bound.
A program may use at most 128 MiB of HBM per device.

v0:
```python
import jax
import jax.numpy as jnp
from jax import lax
from jax.sharding import PartitionSpec as P


def on_device(blocks, block_rows, block_cols, counts, features):
    feature_width = features.shape[1]
    block_size = blocks.shape[-1]
    max_blocks = blocks.shape[2]
    group_size = max_blocks // 8
    row_blocks = lax.axis_size("col") * (features.shape[0] // block_size)
    panel_rows = lax.all_gather(features, "row", axis=0, tiled=True)
    panel_blocks = panel_rows.reshape(-1, block_size, feature_width)
    tile_blocks = blocks[0, 0]
    tile_rows = block_rows[0, 0]
    tile_cols = block_cols[0, 0]
    live_count = counts[0, 0]

    def accumulate(group_index, running):
        first_slot = group_index * group_size
        weights = lax.dynamic_slice_in_dim(tile_blocks, first_slot, group_size, 0)
        rows_slice = lax.dynamic_slice_in_dim(tile_rows, first_slot, group_size, 0)
        cols_slice = lax.dynamic_slice_in_dim(tile_cols, first_slot, group_size, 0)
        positions = first_slot + jnp.arange(group_size, dtype=jnp.int32)
        weights = jnp.where(
            (positions < live_count)[:, None, None], weights, jnp.zeros_like(weights)
        )
        gathered = panel_blocks[cols_slice, :, 0:feature_width]
        product = jnp.einsum("gik,gkf->gif", weights, gathered, preferred_element_type=jnp.float32)
        return running.at[rows_slice].add(product)

    initial = jnp.zeros((row_blocks, block_size, feature_width - 0), jnp.float32)
    groups = 8
    running = lax.fori_loop(0, groups, accumulate, initial)
    return lax.psum_scatter(
        running.reshape(row_blocks * block_size, feature_width - 0).astype(jnp.bfloat16),
        "col",
        scatter_dimension=0,
        tiled=True,
    )


def solution(mesh):
    return jax.shard_map(
        on_device,
        mesh=mesh,
        in_specs=(
            P("row", "col", None, None, None),
            P("row", "col", None),
            P("row", "col", None),
            P("row", "col"),
            P(("col", "row"), None),
        ),
        out_specs=P(("row", "col"), None),
        check_vma=False,
    )
```

profile of v0, /device:TPU:0, one launch (start us, length us, event | category | flops | bytes accessed | tf_op | source)
XLA Modules:
  0.0 290.4 jit_solution(15859293063505907300)
XLA Ops:
  6.5 0.7 all-gather.2.cloned.1.call-update
  7.3 0.7 reduce
  8.0 0.7 reduce.1
  8.7 39.9 %all-gather.2.cloned.1.call-done = bf16[8192,256]{1,0:T(8,128)(2,1)} async-done(((bf16[1024,256]{1,0:T(8,128)(2,1)}), bf16[8192,256]{1,0:T(8,128)(2,1)}) %all-gather.2.cloned.1.call-update) | async-done | bytes 4194320 | tf_op jit(solution)/shard_map/all_gather | solution.py:13
  48.6 2.6 broadcast_in_dim.38
  51.1 184.6 %while.13 = (s32[]{:T(128)}, f32[32,128,256]{2,1,0:T(8,128)}, s32[368]{0:T(512)S(1)}, s32[]{:T(128)}, bf16[368,128,128]{2,1,0:T(8,128)(2,1)}, /*index=5*/s32[368...) while((s32[]{:T(128)}, f32[32,128,256]{2,1,0:T(8,128)}, ...), condition=%wide.region_2.3_spmd, body=%wide.region_0.2_spmd.sunk | while | flops 388138368 | bytes 34674192 | solution.py:35
  51.9 2.9 %gather_fusion = bf16[46,128,256]{2,1,0:T(8,128)(2,1)S(1)} fusion(bf16[64,128,256]{2,1,0:T(8,128)(2,1)} %get-tuple-element.221, s32[1024]{0:T(1024)S(1)} %pad_clamp_fusion.2), kind=kCustom, calls=%fused_computation.clone.1 | custom fusion | bytes 6029496 | tf_op jit(solution)/shard_map/while/body/eval_jaxpr/gather | solution.py:29
  54.8 5.0 %fusion.13 = f32[46,128,256]{2,1,0:T(8,128)} fusion(bf16[46,128,256]{2,1,0:T(8,128)(2,1)S(1)} %gather_fusion, bf16[368,128,128]{2,1,0:T(8,128)(2,1)} %get-tuple-element.219, s32[]{:T(128)S(6)} %select_n.40, pred[46]{0:T(512)(128)(4,1)S(1)} %add_compare_fusion.2), kind=kOutput, calls=%fused_computation.2.clone.1 | convolution fusion | flops 386629632 | bytes 10551346 | tf_op jit(solution)/shard_map/while/body/eval_jaxpr/gik,gkf->gif/dot_general | solution.py:30
  59.8 14.5 %scatter_fusion = f32[32,128,256]{2,1,0:T(8,128)} fusion(f32[32,128,256]{2,1,0:T(8,128)} %get-tuple-element.205, s32[46]{0:T(128)S(1)} %get-tuple-element.191, f32[46,128,256]{2,1,0:T(8,128)} %fusion.13), kind=kCustom, calls=%fused_computation.1.clone.1 | custom fusion | flops 1507328 | bytes 18088120 | tf_op jit(solution)/shard_map/while/body/eval_jaxpr/scatter-add | solution.py:31
  75.0 2.9 %gather_fusion = bf16[46,128,256]{2,1,0:T(8,128)(2,1)S(1)} fusion(bf16[64,128,256]{2,1,0:T(8,128)(2,1)} %get-tuple-element.221, s32[1024]{0:T(1024)S(1)} %pad_clamp_fusion.2), kind=kCustom, calls=%fused_computation.clone.1 | custom fusion | bytes 6029496 | tf_op jit(solution)/shard_map/while/body/eval_jaxpr/gather | solution.py:29
  77.9 5.0 %fusion.13 = f32[46,128,256]{2,1,0:T(8,128)} fusion(bf16[46,128,256]{2,1,0:T(8,128)(2,1)S(1)} %gather_fusion, bf16[368,128,128]{2,1,0:T(8,128)(2,1)} %get-tuple-element.219, s32[]{:T(128)S(6)} %select_n.40, pred[46]{0:T(512)(128)(4,1)S(1)} %add_compare_fusion.2), kind=kOutput, calls=%fused_computation.2.clone.1 | convolution fusion | flops 386629632 | bytes 10551346 | tf_op jit(solution)/shard_map/while/body/eval_jaxpr/gik,gkf->gif/dot_general | solution.py:30
  82.8 14.5 %scatter_fusion = f32[32,128,256]{2,1,0:T(8,128)} fusion(f32[32,128,256]{2,1,0:T(8,128)} %get-tuple-element.205, s32[46]{0:T(128)S(1)} %get-tuple-element.191, f32[46,128,256]{2,1,0:T(8,128)} %fusion.13), kind=kCustom, calls=%fused_computation.1.clone.1 | custom fusion | flops 1507328 | bytes 18088120 | tf_op jit(solution)/shard_map/while/body/eval_jaxpr/scatter-add | solution.py:31
  98.1 2.9 %gather_fusion = bf16[46,128,256]{2,1,0:T(8,128)(2,1)S(1)} fusion(bf16[64,128,256]{2,1,0:T(8,128)(2,1)} %get-tuple-element.221, s32[1024]{0:T(1024)S(1)} %pad_clamp_fusion.2), kind=kCustom, calls=%fused_computation.clone.1 | custom fusion | bytes 6029496 | tf_op jit(solution)/shard_map/while/body/eval_jaxpr/gather | solution.py:29
  101.0 5.0 %fusion.13 = f32[46,128,256]{2,1,0:T(8,128)} fusion(bf16[46,128,256]{2,1,0:T(8,128)(2,1)S(1)} %gather_fusion, bf16[368,128,128]{2,1,0:T(8,128)(2,1)} %get-tuple-element.219, s32[]{:T(128)S(6)} %select_n.40, pred[46]{0:T(512)(128)(4,1)S(1)} %add_compare_fusion.2), kind=kOutput, calls=%fused_computation.2.clone.1 | convolution fusion | flops 386629632 | bytes 10551346 | tf_op jit(solution)/shard_map/while/body/eval_jaxpr/gik,gkf->gif/dot_general | solution.py:30
  106.0 14.6 %scatter_fusion = f32[32,128,256]{2,1,0:T(8,128)} fusion(f32[32,128,256]{2,1,0:T(8,128)} %get-tuple-element.205, s32[46]{0:T(128)S(1)} %get-tuple-element.191, f32[46,128,256]{2,1,0:T(8,128)} %fusion.13), kind=kCustom, calls=%fused_computation.1.clone.1 | custom fusion | flops 1507328 | bytes 18088120 | tf_op jit(solution)/shard_map/while/body/eval_jaxpr/scatter-add | solution.py:31
  121.3 2.9 %gather_fusion = bf16[46,128,256]{2,1,0:T(8,128)(2,1)S(1)} fusion(bf16[64,128,256]{2,1,0:T(8,128)(2,1)} %get-tuple-element.221, s32[1024]{0:T(1024)S(1)} %pad_clamp_fusion.2), kind=kCustom, calls=%fused_computation.clone.1 | custom fusion | bytes 6029496 | tf_op jit(solution)/shard_map/while/body/eval_jaxpr/gather | solution.py:29
  124.3 5.0 %fusion.13 = f32[46,128,256]{2,1,0:T(8,128)} fusion(bf16[46,128,256]{2,1,0:T(8,128)(2,1)S(1)} %gather_fusion, bf16[368,128,128]{2,1,0:T(8,128)(2,1)} %get-tuple-element.219, s32[]{:T(128)S(6)} %select_n.40, pred[46]{0:T(512)(128)(4,1)S(1)} %add_compare_fusion.2), kind=kOutput, calls=%fused_computation.2.clone.1 | convolution fusion | flops 386629632 | bytes 10551346 | tf_op jit(solution)/shard_map/while/body/eval_jaxpr/gik,gkf->gif/dot_general | solution.py:30
  129.2 14.4 %scatter_fusion = f32[32,128,256]{2,1,0:T(8,128)} fusion(f32[32,128,256]{2,1,0:T(8,128)} %get-tuple-element.205, s32[46]{0:T(128)S(1)} %get-tuple-element.191, f32[46,128,256]{2,1,0:T(8,128)} %fusion.13), kind=kCustom, calls=%fused_computation.1.clone.1 | custom fusion | flops 1507328 | bytes 18088120 | tf_op jit(solution)/shard_map/while/body/eval_jaxpr/scatter-add | solution.py:31
  144.3 2.9 %gather_fusion = bf16[46,128,256]{2,1,0:T(8,128)(2,1)S(1)} fusion(bf16[64,128,256]{2,1,0:T(8,128)(2,1)} %get-tuple-element.221, s32[1024]{0:T(1024)S(1)} %pad_clamp_fusion.2), kind=kCustom, calls=%fused_computation.clone.1 | custom fusion | bytes 6029496 | tf_op jit(solution)/shard_map/while/body/eval_jaxpr/gather | solution.py:29
  147.3 5.0 %fusion.13 = f32[46,128,256]{2,1,0:T(8,128)} fusion(bf16[46,128,256]{2,1,0:T(8,128)(2,1)S(1)} %gather_fusion, bf16[368,128,128]{2,1,0:T(8,128)(2,1)} %get-tuple-element.219, s32[]{:T(128)S(6)} %select_n.40, pred[46]{0:T(512)(128)(4,1)S(1)} %add_compare_fusion.2), kind=kOutput, calls=%fused_computation.2.clone.1 | convolution fusion | flops 386629632 | bytes 10551346 | tf_op jit(solution)/shard_map/while/body/eval_jaxpr/gik,gkf->gif/dot_general | solution.py:30
  152.2 14.3 %scatter_fusion = f32[32,128,256]{2,1,0:T(8,128)} fusion(f32[32,128,256]{2,1,0:T(8,128)} %get-tuple-element.205, s32[46]{0:T(128)S(1)} %get-tuple-element.191, f32[46,128,256]{2,1,0:T(8,128)} %fusion.13), kind=kCustom, calls=%fused_computation.1.clone.1 | custom fusion | flops 1507328 | bytes 18088120 | tf_op jit(solution)/shard_map/while/body/eval_jaxpr/scatter-add | solution.py:31
  167.3 2.9 %gather_fusion = bf16[46,128,256]{2,1,0:T(8,128)(2,1)S(1)} fusion(bf16[64,128,256]{2,1,0:T(8,128)(2,1)} %get-tuple-element.221, s32[1024]{0:T(1024)S(1)} %pad_clamp_fusion.2), kind=kCustom, calls=%fused_computation.clone.1 | custom fusion | bytes 6029496 | tf_op jit(solution)/shard_map/while/body/eval_jaxpr/gather | solution.py:29
  170.2 5.0 %fusion.13 = f32[46,128,256]{2,1,0:T(8,128)} fusion(bf16[46,128,256]{2,1,0:T(8,128)(2,1)S(1)} %gather_fusion, bf16[368,128,128]{2,1,0:T(8,128)(2,1)} %get-tuple-element.219, s32[]{:T(128)S(6)} %select_n.40, pred[46]{0:T(512)(128)(4,1)S(1)} %add_compare_fusion.2), kind=kOutput, calls=%fused_computation.2.clone.1 | convolution fusion | flops 386629632 | bytes 10551346 | tf_op jit(solution)/shard_map/while/body/eval_jaxpr/gik,gkf->gif/dot_general | solution.py:30
  175.2 14.4 %scatter_fusion = f32[32,128,256]{2,1,0:T(8,128)} fusion(f32[32,128,256]{2,1,0:T(8,128)} %get-tuple-element.205, s32[46]{0:T(128)S(1)} %get-tuple-element.191, f32[46,128,256]{2,1,0:T(8,128)} %fusion.13), kind=kCustom, calls=%fused_computation.1.clone.1 | custom fusion | flops 1507328 | bytes 18088120 | tf_op jit(solution)/shard_map/while/body/eval_jaxpr/scatter-add | solution.py:31
  190.3 2.9 %gather_fusion = bf16[46,128,256]{2,1,0:T(8,128)(2,1)S(1)} fusion(bf16[64,128,256]{2,1,0:T(8,128)(2,1)} %get-tuple-element.221, s32[1024]{0:T(1024)S(1)} %pad_clamp_fusion.2), kind=kCustom, calls=%fused_computation.clone.1 | custom fusion | bytes 6029496 | tf_op jit(solution)/shard_map/while/body/eval_jaxpr/gather | solution.py:29
  193.2 5.0 %fusion.13 = f32[46,128,256]{2,1,0:T(8,128)} fusion(bf16[46,128,256]{2,1,0:T(8,128)(2,1)S(1)} %gather_fusion, bf16[368,128,128]{2,1,0:T(8,128)(2,1)} %get-tuple-element.219, s32[]{:T(128)S(6)} %select_n.40, pred[46]{0:T(512)(128)(4,1)S(1)} %add_compare_fusion.2), kind=kOutput, calls=%fused_computation.2.clone.1 | convolution fusion | flops 386629632 | bytes 10551346 | tf_op jit(solution)/shard_map/while/body/eval_jaxpr/gik,gkf->gif/dot_general | solution.py:30
  198.2 14.5 %scatter_fusion = f32[32,128,256]{2,1,0:T(8,128)} fusion(f32[32,128,256]{2,1,0:T(8,128)} %get-tuple-element.205, s32[46]{0:T(128)S(1)} %get-tuple-element.191, f32[46,128,256]{2,1,0:T(8,128)} %fusion.13), kind=kCustom, calls=%fused_computation.1.clone.1 | custom fusion | flops 1507328 | bytes 18088120 | tf_op jit(solution)/shard_map/while/body/eval_jaxpr/scatter-add | solution.py:31
  213.5 2.9 %gather_fusion = bf16[46,128,256]{2,1,0:T(8,128)(2,1)S(1)} fusion(bf16[64,128,256]{2,1,0:T(8,128)(2,1)} %get-tuple-element.221, s32[1024]{0:T(1024)S(1)} %pad_clamp_fusion.2), kind=kCustom, calls=%fused_computation.clone.1 | custom fusion | bytes 6029496 | tf_op jit(solution)/shard_map/while/body/eval_jaxpr/gather | solution.py:29
  216.4 5.0 %fusion.13 = f32[46,128,256]{2,1,0:T(8,128)} fusion(bf16[46,128,256]{2,1,0:T(8,128)(2,1)S(1)} %gather_fusion, bf16[368,128,128]{2,1,0:T(8,128)(2,1)} %get-tuple-element.219, s32[]{:T(128)S(6)} %select_n.40, pred[46]{0:T(512)(128)(4,1)S(1)} %add_compare_fusion.2), kind=kOutput, calls=%fused_computation.2.clone.1 | convolution fusion | flops 386629632 | bytes 10551346 | tf_op jit(solution)/shard_map/while/body/eval_jaxpr/gik,gkf->gif/dot_general | solution.py:30
  221.4 14.4 %scatter_fusion = f32[32,128,256]{2,1,0:T(8,128)} fusion(f32[32,128,256]{2,1,0:T(8,128)} %get-tuple-element.205, s32[46]{0:T(128)S(1)} %get-tuple-element.191, f32[46,128,256]{2,1,0:T(8,128)} %fusion.13), kind=kCustom, calls=%fused_computation.1.clone.1 | custom fusion | flops 1507328 | bytes 18088120 | tf_op jit(solution)/shard_map/while/body/eval_jaxpr/scatter-add | solution.py:31
  235.7 3.8 %convert_element_type.6 = bf16[32,128,256]{2,1,0:T(8,128)(2,1)} convert(f32[32,128,256]{2,1,0:T(8,128)} %get-tuple-element.129) | non-fusion elementwise | flops 1048576 | bytes 6291456 | tf_op jit(solution)/shard_map/convert_element_type | solution.py:37
  239.6 44.0 %reduce-scatter.2.cloned.1.call-done = bf16[1024,256]{1,0:T(8,128)(2,1)} async-done(((bf16[4096,256]{1,0:T(8,128)(2,1)}), bf16[1024,256]{1,0:T(8,128)(2,1)}) %reduce-scatter.2.cloned.1.call-update) | async-done | bytes 524304 | tf_op jit(solution)/shard_map/reduce_scatter | solution.py:36
  (27 shorter events, 6.0 us)
Async XLA Ops:
  6.5 42.0 %all-gather.2.cloned.1.call-start = ((), (), s32[]{:S(2)}) async-start(), calls=%async_computation.1 | async-start | bytes 4718592 | tf_op jit(solution)/shard_map/all_gather | solution.py:13
  7.3 276.3 %reduce-scatter.2.cloned.1.call-start = ((), (), s32[]{:S(2)}) async-start(), calls=%async_computation.2 | async-start | bytes 2621440 | tf_op jit(solution)/shard_map/reduce_scatter | solution.py:36
Sparse Core Ops, SparseCore 0:
  9.2 39.2 all-gather.1
  239.7 43.7 reduce-scatter.1
where the time goes:
time: 292 us; the launch traced here: 290 us
  other arithmetic  127 us (43%)
  waiting for transfers between devices  84.5 us (29%)
  matrix products  39.6 us (14%)
  local copies, waits for them, and re-layouts  26 us (9%)
  between operations  13.4 us (5%)
    scatter-add x8, other arithmetic, accumulate(): return running.at[rows_slice].add(product)  116 us
    reduce_scatter x1, waiting for transfers between devices, on_device(): lax.psum_scatter(running.reshape(row_blocks * block_size, feature_width -...  44 us
    all_gather x1, waiting for transfers between devices, on_device(): panel_rows = lax.all_gather(features, 'row', axis=0, tiled=True)  39.9 us
    dot_general x8, matrix products, accumulate(): jnp.einsum('gik,gkf->gif', weights, gathered, preferred_element_type=jnp....  39.6 us
    gather x8, local copies, waits for them, and re-layouts, accumulate(): gathered = panel_blocks[cols_slice, :, 0:feature_width]  23.4 us
  transfers between devices with their start and end apart: 2, of which 2 were waited for; matrix products, arithmetic and copies ran while one was open for 0% of the time, Pallas kernels for 0%

commit v1 on v0

v1 whole, which is shorter than its diff:
```python
import functools

import jax
import jax.numpy as jnp
from jax import lax
from jax.experimental import pallas as pl
from jax.experimental.pallas import tpu as pltpu
from jax.sharding import PartitionSpec as P

MESH = pl.DeviceIdType.MESH
LANES = 128
HALVES = 2


def bits_for(extent):
    return max(1, (extent - 1).bit_length())


def slot_plan(tile_rows, tile_cols, live_count, row_blocks, slot_bits, col_bits):
    slots = tile_rows.shape[0]
    position = jnp.arange(slots, dtype=jnp.int32)
    row = jnp.where(position < live_count, tile_rows, row_blocks)
    key = (row << slot_bits) + position
    rank = jnp.sum((key[None, :] < key[:, None]).astype(jnp.int32), axis=1)
    packed = (key << col_bits) + tile_cols
    ordered = jnp.sum(jnp.where(rank[:, None] == position[None, :], packed[:, None], 0), axis=0)
    wanted = jnp.arange(row_blocks, dtype=jnp.int32)
    upto = jnp.sum((row[:, None] <= wanted[None, :]).astype(jnp.int32), axis=0)
    here = jnp.sum((row[:, None] == wanted[None, :]).astype(jnp.int32), axis=0)
    last = jnp.where(here > 0, upto - 1, -1)
    return ordered, last


def kernel(
    n_row, n_col, row_blocks, slot_bits, col_bits,
    ordered, last, blocks_hbm, features_hbm, out,
    held, panel0, panel1, sums, part0, part1, right0, right1, left0, left1,
    load_sem, ag_send, ag_recv, rs_send, rs_recv,
):
    panels, parts = (panel0, panel1), (part0, part1)
    rights, lefts = (right0, right1), (left0, left1)
    slots = held.shape[0]
    owned = panel0.shape[0] // n_row
    chunk = row_blocks // n_col
    me = lax.axis_index("row")
    p = lax.axis_index("col")

    fetch = pltpu.make_async_copy(blocks_hbm, held, load_sem.at[HALVES])
    mine = [
        pltpu.make_async_copy(
            features_hbm.at[:, :, pl.ds(h * LANES, LANES)],
            panels[h].at[pl.ds(me * owned, owned)],
            load_sem.at[h],
        )
        for h in range(HALVES)
    ]
    for copy in mine:
        copy.start()
    fetch.start()

    cube = n_row == 8
    core = lax.rem(me, 2)
    if cube:
        x_bit = lax.rem(me // 2, 2)
        y_bit = me // 4
        other = me + 1 - 2 * core
        beside = me + 2 - 4 * x_bit
        above = me + 4 - 8 * y_bit
        across = beside + 4 - 8 * y_bit
        flip = 1 - 2 * core
        mates = [other, beside, above]
    else:
        mates = [lax.rem(me + k, n_row) for k in range(1, n_row)]

    barrier = pltpu.get_barrier_semaphore()
    for mate in mates:
        pl.semaphore_signal(barrier, inc=1, device_id=(mate, p), device_id_type=MESH)

    @pl.when(p > 0)
    def _():
        pl.semaphore_signal(barrier, inc=1, device_id=(me, p - 1), device_id_type=MESH)

    @pl.when(p < n_col - 1)
    def _():
        pl.semaphore_signal(barrier, inc=1, device_id=(me, p + 1), device_id_type=MESH)

    inner = jnp.logical_and(p > 0, p < n_col - 1)

    @pl.when(inner)
    def _():
        pl.semaphore_wait(barrier, len(mates) + 2)

    @pl.when(jnp.logical_not(inner))
    def _():
        pl.semaphore_wait(barrier, len(mates) + 1)

    def shard_copy(h, shard, target, send, recv):
        where = panels[h].at[pl.ds(shard * owned, owned)]
        return pltpu.make_async_remote_copy(
            src_ref=where,
            dst_ref=where,
            send_sem=ag_send.at[h, send],
            recv_sem=ag_recv.at[h, recv],
            device_id=(target, p),
            device_id_type=MESH,
        )

    if cube:
        def first_sends(h):
            shard_copy(h, me, beside, 0, 0).start()
            shard_copy(h, me, above, 1, 1).start()
            shard_copy(h, me, other, 2, 3).start()

        def forward(h):
            @pl.when(core == 0)
            def _():
                shard_copy(h, above, me, 1, 1).wait_recv()
                shard_copy(h, above, beside, 3, 2).start()
                shard_copy(h, above, other, 5, 5).start()
                shard_copy(h, beside, me, 0, 0).wait_recv()
                shard_copy(h, beside, other, 4, 4).start()

            @pl.when(core == 1)
            def _():
                shard_copy(h, beside, me, 0, 0).wait_recv()
                shard_copy(h, beside, above, 3, 2).start()
                shard_copy(h, beside, other, 4, 4).start()
                shard_copy(h, above, me, 1, 1).wait_recv()
                shard_copy(h, above, other, 5, 5).start()

        def gathered(h):
            shard_copy(h, across, me, 2, 2).wait_recv()
            shard_copy(h, across, other, 6, 6).start()
            shard_copy(h, other, me, 2, 3).wait_recv()
            shard_copy(h, beside + flip, me, 4, 4).wait_recv()
            shard_copy(h, above + flip, me, 5, 5).wait_recv()
            shard_copy(h, across + flip, me, 6, 6).wait_recv()

        sends = 7
    else:
        def first_sends(h):
            for k in range(1, n_row):
                shard_copy(h, me, lax.rem(me + k, n_row), k - 1, k - 1).start()

        def forward(h):
            pass

        def gathered(h):
            for k in range(1, n_row):
                shard_copy(h, lax.rem(me + n_row - k, n_row), me, k - 1, k - 1).wait_recv()

        sends = n_row - 1

    def compute(h):
        unroll = 8 if slots % 8 == 0 else 1

        def step(group, carry):
            total, before = carry
            for u in range(unroll):
                place = group * unroll + u
                word = ordered[place]
                row = word >> (slot_bits + col_bits)
                slot = (word >> col_bits) & ((1 << slot_bits) - 1)
                col = word & ((1 << col_bits) - 1)
                product = jnp.dot(held[slot], panels[h][col], preferred_element_type=jnp.float32)
                total = jnp.where(row == before, total, 0.0) + product
                sums[place] = total.astype(jnp.bfloat16)
                before = row
            return total, before

        zero = jnp.zeros((held.shape[1], LANES), jnp.float32)
        lax.fori_loop(0, slots // unroll, step, (zero, jnp.int32(-1)))

        def pick(i, _):
            place = last[i]
            value = sums[jnp.maximum(place, 0)]
            parts[h][i] = jnp.where(place >= 0, value, jnp.zeros_like(value))
            return 0

        lax.fori_loop(0, row_blocks, pick, 0)

    def rs_copy(h, side, d, source):
        land = (rights, lefts)[side][h]
        return pltpu.make_async_remote_copy(
            src_ref=source,
            dst_ref=land.at[d],
            send_sem=rs_send.at[h, side, d],
            recv_sem=rs_recv.at[h, side, d],
            device_id=(me, p + 1 - 2 * side),
            device_id_type=MESH,
        )

    def own(h, d):
        return parts[h].at[pl.ds(d * chunk, chunk)]

    def start_ends(h):
        @pl.when(p == 0)
        def _():
            for d in range(n_col - 1, 0, -1):
                rs_copy(h, 0, d, own(h, d)).start()

        @pl.when(p == n_col - 1)
        def _():
            for d in range(n_col - 1):
                rs_copy(h, 1, d, own(h, d)).start()

    def pass_on(h, side, d):
        land = (rights, lefts)[side][h]
        rs_copy(h, side, d, land.at[d]).wait_recv()

        def add(k, _):
            land[d, k] = (
                land[d, k].astype(jnp.float32) + parts[h][d * chunk + k].astype(jnp.float32)
            ).astype(jnp.bfloat16)
            return 0

        lax.fori_loop(0, chunk, add, 0)
        rs_copy(h, side, d, land.at[d]).start()

    def relay(h):
        for k in range(n_col - 1):
            d = n_col - 1 - k

            @pl.when(jnp.logical_and(p > 0, p < d))
            def _():
                pass_on(h, 0, d)

            @pl.when(jnp.logical_and(p > k, p < n_col - 1))
            def _():
                pass_on(h, 1, k)

    def finish(h):
        cols = pl.ds(h * LANES, LANES)

        def total(from_left, from_right):
            if from_left:
                rs_copy(h, 0, p, rights[h].at[p]).wait_recv()
            if from_right:
                rs_copy(h, 1, p, lefts[h].at[p]).wait_recv()

            def add(k, _):
                value = parts[h][p * chunk + k].astype(jnp.float32)
                if from_left:
                    value = value + rights[h][p, k].astype(jnp.float32)
                if from_right:
                    value = value + lefts[h][p, k].astype(jnp.float32)
                out[k, :, cols] = value.astype(jnp.bfloat16)
                return 0

            lax.fori_loop(0, chunk, add, 0)

        pl.when(p == 0)(lambda: total(False, True))
        pl.when(p == n_col - 1)(lambda: total(True, False))
        pl.when(jnp.logical_and(p > 0, p < n_col - 1))(lambda: total(True, True))

    for h in range(HALVES):
        mine[h].wait()
        first_sends(h)
    forward(0)
    gathered(0)
    fetch.wait()
    compute(0)
    start_ends(0)
    forward(1)
    gathered(1)
    compute(1)
    start_ends(1)
    for h in range(HALVES):
        relay(h)
        finish(h)

    for h in range(HALVES):
        for k in range(sends):
            shard_copy(h, me, me, k, 0).wait_send()
        for d in range(n_col):
            @pl.when(p < d)
            def _():
                rs_copy(h, 0, d, own(h, d)).wait_send()

            @pl.when(p > d)
            def _():
                rs_copy(h, 1, d, own(h, d)).wait_send()


def on_device(n_row, n_col, blocks, block_rows, block_cols, counts, features):
    nodes, width = features.shape
    slots, size = blocks.shape[2], blocks.shape[-1]
    owned = nodes // size
    row_blocks = n_col * owned
    panel_blocks = n_row * owned
    slot_bits, col_bits = bits_for(slots), bits_for(panel_blocks)
    ordered, last = slot_plan(
        block_rows[0, 0], block_cols[0, 0], counts[0, 0], row_blocks, slot_bits, col_bits
    )
    half = (size, LANES)
    vmem = lambda *lead: pltpu.VMEM((*lead, *half), jnp.bfloat16)
    smem = pl.BlockSpec(memory_space=pltpu.SMEM)
    hbm = pl.BlockSpec(memory_space=pl.ANY)
    result = pl.pallas_call(
        functools.partial(kernel, n_row, n_col, row_blocks, slot_bits, col_bits),
        out_shape=jax.ShapeDtypeStruct((owned, size, width), jnp.bfloat16),
        in_specs=[smem, smem, hbm, hbm],
        out_specs=pl.BlockSpec(memory_space=pltpu.VMEM),
        scratch_shapes=[
            pltpu.VMEM((slots, size, size), jnp.bfloat16),
            vmem(panel_blocks), vmem(panel_blocks),
            vmem(slots),
            vmem(row_blocks), vmem(row_blocks),
            vmem(n_col, owned), vmem(n_col, owned), vmem(n_col, owned), vmem(n_col, owned),
            pltpu.SemaphoreType.DMA((HALVES + 1,)),
            pltpu.SemaphoreType.DMA((HALVES, max(7, n_row - 1))),
            pltpu.SemaphoreType.DMA((HALVES, max(7, n_row - 1))),
            pltpu.SemaphoreType.DMA((HALVES, 2, n_col)),
            pltpu.SemaphoreType.DMA((HALVES, 2, n_col)),
        ],
        compiler_params=pltpu.CompilerParams(
            collective_id=0, has_side_effects=True, vmem_limit_bytes=67043328
        ),
    )(ordered, last, blocks.reshape(slots, size, size), features.reshape(owned, size, width))
    return result.reshape(nodes, width)


def solution(mesh):
    return jax.shard_map(
        functools.partial(on_device, mesh.shape["row"], mesh.shape["col"]),
        mesh=mesh,
        in_specs=(
            P("row", "col", None, None, None),
            P("row", "col", None),
            P("row", "col", None),
            P("row", "col"),
            P(("col", "row"), None),
        ),
        out_specs=P(("row", "col"), None),
        check_vma=False,
    )
```

time: 292 us -> 99.4 us (0.34)
  other arithmetic: 127 us -> 3.12 us
  Pallas kernels: 0 us -> 93.6 us
  waiting for transfers between devices: 84.5 us -> 0 us
  matrix products: 39.6 us -> 0 us
  local copies, waits for them, and re-layouts: 26 us -> 1.87 us
  between operations: 13.4 us -> 0.67 us
    scatter-add x8 -> x0, other arithmetic: 116 us -> none  [accumulate(): return running.at[rows_slice].add(product)]
    pallas_call x0 -> x1, Pallas kernels: none -> 93.6 us  [on_device(): pl.pallas_call(functools.partial(kernel, n_row, n_col, row_blocks, slot_b...]
    reduce_scatter x1 -> x0, waiting for transfers between devices: 44 us -> none  [on_device(): lax.psum_scatter(running.reshape(row_blocks * block_size, feature_width -...]
    all_gather x1 -> x0, waiting for transfers between devices: 39.9 us -> none  [on_device(): panel_rows = lax.all_gather(features, 'row', axis=0, tiled=True)]
    dot_general x8 -> x0, matrix products: 39.6 us -> none  [accumulate(): jnp.einsum('gik,gkf->gif', weights, gathered, preferred_element_type=jnp....]
    gather x8 -> x0, local copies, waits for them, and re-layouts: 23.4 us -> none  [accumulate(): gathered = panel_blocks[cols_slice, :, 0:feature_width]]
    lt x8 -> x0, other arithmetic: 5.2 us -> none  [accumulate(): positions < live_count]
    convert_element_type x1 -> x0, other arithmetic: 3.83 us -> none  [on_device(): running.reshape(row_blocks * block_size, feature_width - 0)]
  transfers between devices with their start and end apart: 2 -> 0, of which waited for: 2 -> 0; matrix products, arithmetic and copies ran while one was open for 0% -> 0% of each run, Pallas kernels for 0% -> 0%
where the time goes in v1:
time: 99.4 us; the launch traced here: 99.2 us
  Pallas kernels  93.6 us (94%)
  other arithmetic  3.12 us (3%)
  local copies, waits for them, and re-layouts  1.87 us (2%)
    pallas_call x1, Pallas kernels, on_device(): pl.pallas_call(functools.partial(kernel, n_row, n_col, row_blocks, slot_b...  93.6 us

profile of v1, /device:TPU:0, one launch (start us, length us, event | category | flops | bytes accessed | tf_op | source)
XLA Modules:
  0.0 99.2 jit_solution(16638646928978608114)
XLA Ops:
  0.7 0.7 reduce
  1.4 0.2 convert_reduce_fusion
  1.6 0.1 convert_reduce_fusion.1
  1.7 0.6 compare_select_fusion.last
  2.3 0.7 reduce.1
  3.0 0.8 select_reduce_fusion.ordered
  3.8 93.6 %shard_map.55 = bf16[8,128,256]{2,1,0:T(8,128)(2,1)} custom-call(s32[368]{0:T(512)} %select_reduce_fusion.ordered, s32[32]{0:T(128)} %compare_select_fusion.last, bf16[368,128,128]{2,1,0:T(8,128)(2,1)} %bitcast.5, bf16[8,128,256]{2,1,0:T(8,128)(2,1)} %bitcast.7), custom_call_target="tpu_custom_call" | custom-call | tf_op jit(solution)/shard_map/pallas_call | solution.py:299
  97.3 1.9 %copy.8 = bf16[1024,256]{1,0:T(8,128)(2,1)} copy(bf16[1024,256]{1,0:T(8,128)(2,1)} %bitcast.6) | data formatting | bytes 1048576
  (2 shorter events, 0.0 us)

commit v2 on v1

--- a/solution.py
+++ b/solution.py
@@ -221,11 +221,18 @@
         for k in range(n_col - 1):
             d = n_col - 1 - k
 
+            relays_left = jnp.logical_and(p > k, p < n_col - 1)
+            near_end = p >= n_col // 2
+
+            @pl.when(jnp.logical_and(relays_left, near_end))
+            def _():
+                pass_on(h, 1, k)
+
             @pl.when(jnp.logical_and(p > 0, p < d))
             def _():
                 pass_on(h, 0, d)
 
-            @pl.when(jnp.logical_and(p > k, p < n_col - 1))
+            @pl.when(jnp.logical_and(relays_left, jnp.logical_not(near_end)))
             def _():
                 pass_on(h, 1, k)
 
@@ -253,10 +260,11 @@
         pl.when(p == n_col - 1)(lambda: total(True, False))
         pl.when(jnp.logical_and(p > 0, p < n_col - 1))(lambda: total(True, True))
 
-    for h in range(HALVES):
-        mine[h].wait()
-        first_sends(h)
+    mine[0].wait()
+    first_sends(0)
     forward(0)
+    mine[1].wait()
+    first_sends(1)
     gathered(0)
     fetch.wait()
     compute(0)
@@ -267,6 +275,7 @@
     start_ends(1)
     for h in range(HALVES):
         relay(h)
+    for h in range(HALVES):
         finish(h)
 
     for h in range(HALVES):

time: 99.4 us -> 80.6 us (0.81)
  Pallas kernels: 93.6 us -> 74.7 us
    pallas_call x1, Pallas kernels: 93.6 us -> 74.7 us  [on_device(): pl.pallas_call(functools.partial(kernel, n_row, n_col, row_blocks, slot_b...]
where the time goes in v2:
time: 80.6 us; the launch traced here: 80.3 us
  Pallas kernels  74.7 us (93%)
  other arithmetic  3.12 us (4%)
  local copies, waits for them, and re-layouts  1.87 us (2%)
    pallas_call x1, Pallas kernels, on_device(): pl.pallas_call(functools.partial(kernel, n_row, n_col, row_blocks, slot_b...  74.7 us
    unnamed x1, local copies, waits for them, and re-layouts  1.87 us

profile of v2, /device:TPU:0, one launch (start us, length us, event | category | flops | bytes accessed | tf_op | source)
XLA Modules:
  0.0 80.3 jit_solution(497467699529996267)
XLA Ops:
  0.7 0.7 reduce
  1.4 0.2 convert_reduce_fusion
  1.6 0.1 convert_reduce_fusion.1
  1.7 0.6 compare_select_fusion.last
  2.3 0.7 reduce.1
  3.0 0.8 select_reduce_fusion.ordered
  3.8 74.7 %shard_map.55 = bf16[8,128,256]{2,1,0:T(8,128)(2,1)} custom-call(s32[368]{0:T(512)} %select_reduce_fusion.ordered, s32[32]{0:T(128)} %compare_select_fusion.last, bf16[368,128,128]{2,1,0:T(8,128)(2,1)} %bitcast.5, bf16[8,128,256]{2,1,0:T(8,128)(2,1)} %bitcast.7), custom_call_target="tpu_custom_call" | custom-call | tf_op jit(solution)/shard_map/pallas_call | solution.py:308
  78.5 1.9 %copy.8 = bf16[1024,256]{1,0:T(8,128)(2,1)} copy(bf16[1024,256]{1,0:T(8,128)(2,1)} %bitcast.6) | data formatting | bytes 1048576
  (2 shorter events, 0.0 us)
